TPU v7x, 32 devices: a whole 2x2x4 slice. The times are simulated.
32 devices in a mesh: gx: 4 (over y, x), gy: 2 (over core), gz: 4 (over z).
Axes of the slice: x: 2, y: 2, z: 4, core: 2. Of those that a mesh axis runs over, the one named last changes fastest.
Arguments:
- pair: bfloat16 [128, 1024, 1024], P('gz', 'gy', 'gx'), may hold values from -6 to 6
- pair_mask: int32 [1024, 1024], P('gy', 'gx'), may hold values 0 or 1
- in_gain: float32 [128], replicated, may hold values from 0.5 to 2
- w_left: bfloat16 [128, 128], P(None, 'gz'), may hold values from -0.5 to 0.5
- w_left_gate: bfloat16 [128, 128], P(None, 'gz'), may hold values from -0.5 to 0.5
- w_right: bfloat16 [128, 128], P(None, 'gz'), may hold values from -0.5 to 0.5
- w_right_gate: bfloat16 [128, 128], P(None, 'gz'), may hold values from -0.5 to 0.5
- w_out_gate: bfloat16 [128, 128], P(None, 'gz'), may hold values from -0.5 to 0.5
- out_gain: float32 [128], P('gz'), may hold values from 0.5 to 2
- w_out: bfloat16 [128, 128], P(None, 'gz'), may hold values from -0.5 to 0.5
Outputs:
- update: bfloat16 [128, 1024, 1024], P('gz', 'gy', 'gx')
All inputs are finite; a program needn't handle non-finite values. No bound on the sum of `pair_mask` on one device may be relied on, other than what follows from the above.
Results may differ from a plain program's by a relative error of at most 0.0078.
Values may be sent and summed in bfloat16 or wider, within the bound.
No kernel may reach another device: no remote copies, remote signals or barrier semaphores. Data moves between devices by JAX's collectives and lax.ppermute only.
A program may use at most 192 MiB of HBM per device.

v0:
```python
import jax
import jax.numpy as jnp
from jax import lax
from jax.sharding import PartitionSpec as P

epsilon = 1e-05


def local(
    pair,
    pair_mask,
    in_gain,
    w_left,
    w_left_gate,
    w_right,
    w_right_gate,
    w_out_gate,
    out_gain,
    w_out,
):
    gathered = lax.all_gather(pair, "gz", axis=0, tiled=True).astype(jnp.float32)
    average = jnp.mean(gathered, axis=0)
    centered = gathered - average
    spread = jnp.mean(jnp.square(centered), axis=0)
    normed = (centered * lax.rsqrt(spread + epsilon) * in_gain[:, None, None]).astype(jnp.bfloat16)
    mask_float = pair_mask.astype(jnp.float32)[None]

    def project(weight):
        return jnp.einsum("cik,ch->hik", normed, weight, preferred_element_type=jnp.float32)

    left_rows = (mask_float * jax.nn.sigmoid(project(w_left_gate)) * project(w_left)).astype(
        jnp.bfloat16
    )
    right_rows = (mask_float * jax.nn.sigmoid(project(w_right_gate)) * project(w_right)).astype(
        jnp.bfloat16
    )
    out_gate = jax.nn.sigmoid(
        jnp.einsum("cij,cd->dij", normed, w_out_gate, preferred_element_type=jnp.float32)
    )
    left_group, right_group = (
        lax.all_to_all(left_rows, "gx", split_axis=0, concat_axis=2, tiled=True),
        lax.all_to_all(right_rows, "gx", split_axis=0, concat_axis=2, tiled=True),
    )
    full_product = lax.dot_general(
        left_group,
        lax.all_gather(right_group, "gy", axis=1, tiled=True),
        (((2,), (2,)), ((0,), (0,))),
        preferred_element_type=jnp.float32,
    )
    mixed_sum = lax.all_to_all(full_product, "gx", split_axis=2, concat_axis=0, tiled=True)
    channel_count = lax.axis_size("gz") * mixed_sum.shape[0]
    sum_terms = lax.psum(jnp.sum(mixed_sum, axis=0), "gz")
    mix_average = sum_terms / channel_count
    mix_centered = mixed_sum - mix_average
    mix_spread = lax.psum(jnp.sum(jnp.square(mix_centered), axis=0), "gz") / channel_count
    local_mix = (mix_centered * lax.rsqrt(mix_spread + epsilon) * out_gain[:, None, None]).astype(
        jnp.bfloat16
    )
    normed_mix = lax.all_gather(local_mix, "gz", axis=0, tiled=True)
    projected = jnp.einsum("hij,hd->dij", normed_mix, w_out, preferred_element_type=jnp.float32)
    return (out_gate * projected).astype(jnp.bfloat16)


def solution(mesh):
    placed = (
        P("gz", "gy", "gx"),
        P("gy", "gx"),
        P(),
        P(None, "gz"),
        P(None, "gz"),
        P(None, "gz"),
        P(None, "gz"),
        P(None, "gz"),
        P("gz"),
        P(None, "gz"),
    )
    return jax.shard_map(
        local, mesh=mesh, in_specs=placed, out_specs=P("gz", "gy", "gx"), check_vma=False
    )
```

profile of v0, /device:TPU:0, one launch (start us, length us, event | category | flops | bytes accessed | tf_op | source)
XLA Modules:
  0.0 1984.1 jit_solution(8913950968688597543)
XLA Ops:
  8.4 564.6 %all-gather.4.cloned.1.call-done = bf16[128,512,256]{2,1,0:T(8,128)(2,1)} async-done(((bf16[32,512,256]{2,1,0:T(8,128)(2,1)}), bf16[128,512,256]{2,1,0:T(8,128)(2,1)}) %all-gather.4.cloned.1.call-update) | async-done | bytes 33554448 | tf_op jit(solution)/shard_map/all_gather | solution.py:21
  573.0 11.4 convert_reduce_fusion
  584.5 11.7 fusion.2
  596.2 23.0 %fusion.4 = bf16[128,512,256]{2,1,0:T(8,128)(2,1)} fusion(bf16[128,512,256]{2,1,0:T(8,128)(2,1)} %all-gather.4.cloned.1.call-done, f32[128]{0:T(128)S(1)} %copy-done.4, f32[512,256]{1,0:T(8,128)S(1)} %add_rsqrt_fusion.1, f32[512,256]{1,0:T(8,128)S(1)} %broadcast_multiply_fusion.1), kind=kLoop, calls=%fused_computation.6 | loop fusion | flops 83886080 | bytes 68157952 | tf_op jit(solution)/shard_map/convert_element_type | solution.py:25
  619.3 35.7 %fusion.11 = f32[512,256,32]{1,2,0:T(8,128)} fusion(bf16[128,512,256]{2,1,0:T(8,128)(2,1)} %fusion.4, bf16[128,32]{0,1:T(8,128)(2,1)S(1)} %copy-done), kind=kOutput, calls=%fused_computation.13 | convolution fusion | flops 1073741824 | bytes 50339840 | tf_op jit(solution)/shard_map/cik,ch->hik/dot_general | solution.py:29
  655.0 38.1 %fusion.28 = bf16[32,512,256]{2,0,1:T(8,128)(2,1)} fusion(bf16[128,512,256]{2,1,0:T(8,128)(2,1)} %fusion.4, f32[512,256,32]{1,2,0:T(8,128)} %fusion.11, f32[512,256]{1,0:T(8,128)S(1)} %convert_element_type.23, bf16[128,32]{0,1:T(8,128)(2,1)S(1)} %copy-done.6), kind=kOutput, calls=%fused_computation.32 | convolution fusion | flops 1098907648 | bytes 59252736 | tf_op jit(solution)/shard_map/cik,ch->hik/dot_general | solution.py:29
  704.5 97.4 %all_to_all.54 = bf16[32,512,256]{2,1,0:T(8,128)(2,1)S(1)} all-to-all(bf16[32,512,256]{2,1,0:T(8,128)(2,1)} %copy.27), channel_id=1, replica_groups=mesh['gx'=4,'gy'=2,'gz'=4] {'gx'}, dimensions={0} | all-to-all | bytes 16777216 | tf_op jit(solution)/shard_map/all_to_all | solution.py:42
  809.1 14.3 all_to_all.46
  823.5 37.6 %fusion.7 = f32[512,256,32]{1,2,0:T(8,128)} fusion(bf16[128,512,256]{2,1,0:T(8,128)(2,1)} %fusion.4, bf16[128,32]{0,1:T(8,128)(2,1)S(1)} %copy-done.2), kind=kOutput, calls=%fused_computation.9 | convolution fusion | flops 1073741824 | bytes 50339840 | tf_op jit(solution)/shard_map/cik,ch->hik/dot_general | solution.py:29
  861.2 38.1 %fusion.25 = bf16[32,512,256]{2,0,1:T(8,128)(2,1)} fusion(bf16[128,512,256]{2,1,0:T(8,128)(2,1)} %fusion.4, f32[512,256,32]{1,2,0:T(8,128)} %fusion.7, f32[512,256]{1,0:T(8,128)S(1)} %convert_element_type.23, bf16[128,32]{0,1:T(8,128)(2,1)S(1)} %copy-done.7), kind=kOutput, calls=%fused_computation.31 | convolution fusion | flops 1098907648 | bytes 59252736 | tf_op jit(solution)/shard_map/cik,ch->hik/dot_general | solution.py:29
  899.3 11.4 copy.23
  910.7 94.8 %all_to_all.55 = bf16[32,512,256]{2,1,0:T(8,128)(2,1)S(1)} all-to-all(bf16[32,512,256]{2,1,0:T(8,128)(2,1)} %copy.23), channel_id=1, replica_groups=mesh['gx'=4,'gy'=2,'gz'=4] {'gx'}, dimensions={0} | all-to-all | bytes 16777216 | tf_op jit(solution)/shard_map/all_to_all | solution.py:41
  1012.8 14.3 all_to_all.42
  1027.1 17.0 fusion.37
  1044.0 17.6 copy.29
  1061.6 190.6 %all_to_all.56 = f32[8,512,1024]{1,0,2:T(8,128)} all-to-all(f32[8,512,1024]{1,0,2:T(8,128)} %copy.29), channel_id=1, replica_groups=mesh['gx'=4,'gy'=2,'gz'=4] {'gx'}, dimensions={2} | all-to-all | bytes 33554432 | tf_op jit(solution)/shard_map/all_to_all | solution.py:50
  1252.3 20.2 %copy.30 = f32[8,512,4,256]{3,0,2,1:T(8,128)} copy(f32[8,512,4,256]{1,0,3,2:T(8,128)} %bitcast.52) | data formatting | bytes 33554432 | tf_op jit(solution)/shard_map/all_to_all | solution.py:50
  1282.1 36.2 %all-reduce.3.cloned.1.call-done = f32[512,256]{1,0:T(8,128)} async-done(((f32[512,256]{1,0:T(8,128)}), f32[512,256]{1,0:T(8,128)}) %all-reduce.3.cloned.1.call-update) | async-done | bytes 524304 | tf_op jit(solution)/shard_map/psum | solution.py:52
  1319.3 12.2 fusion.19
  1331.6 38.6 %all-reduce.5.cloned.1.call-done = f32[512,256]{1,0:T(8,128)} async-done(((f32[512,256]{1,0:T(8,128)}), f32[512,256]{1,0:T(8,128)}) %all-reduce.5.cloned.1.call-update) | async-done | bytes 524304 | tf_op jit(solution)/shard_map/psum | solution.py:55
  1382.4 35.8 %fusion.5 = f32[512,256,32]{1,2,0:T(8,128)} fusion(bf16[128,512,256]{2,1,0:T(8,128)(2,1)} %fusion.4, bf16[128,32]{0,1:T(8,128)(2,1)S(1)} %copy-done.3), kind=kOutput, calls=%fused_computation.7 | convolution fusion | flops 1073741824 | bytes 50339840 | tf_op jit(solution)/shard_map/cij,cd->dij/dot_general | solution.py:38
  1418.2 525.5 %all-gather.8.cloned.1.call-done = bf16[128,512,256]{2,0,1:T(8,128)(2,1)} async-done(((bf16[32,512,256]{2,0,1:T(8,128)(2,1)}), bf16[128,512,256]{2,0,1:T(8,128)(2,1)}) %all-gather.8.cloned.1.call-update) | async-done | bytes 33554448 | tf_op jit(solution)/shard_map/all_gather | solution.py:59
  1943.8 21.8 %fusion.24 = bf16[32,512,256]{2,0,1:T(8,128)(2,1)} fusion(bf16[128,512,256]{2,0,1:T(8,128)(2,1)} %all-gather.8.cloned.1.call-done, f32[512,256,32]{1,2,0:T(8,128)} %fusion.5, bf16[128,32]{0,1:T(8,128)(2,1)S(1)} %copy-done.8), kind=kOutput, calls=%fused_computation.30 | convolution fusion | flops 1094713344 | bytes 58728448 | tf_op jit(solution)/shard_map/hij,hd->dij/dot_general | solution.py:60
  1965.6 11.5 copy.31
  (39 shorter events, 50.9 us)
Async XLA Ops:
  6.5 612.8 %copy-start = (bf16[128,32]{0,1:T(8,128)(2,1)S(1)}, bf16[128,32]{0,1:T(8,128)(2,1)}, u32[]{:S(2)}) copy-start(bf16[128,32]{0,1:T(8,128)(2,1)} %param.16) | copy-start | bytes 24580
  6.5 566.5 %all-gather.4.cloned.1.call-start = ((), (), s32[]{:S(2)}) async-start(), calls=%async_computation.3 | async-start | bytes 41943040 | tf_op jit(solution)/shard_map/all_gather | solution.py:21
  7.3 1019.8 %all-gather.6.cloned.1.call-start = ((), (), s32[]{:S(2)}) async-start(), calls=%async_computation.4 | async-start | bytes 25165824 | tf_op jit(solution)/shard_map/all_gather | solution.py:46
  584.5 11.8 copy-start.4
  619.3 35.7 %copy-start.6 = (bf16[128,32]{0,1:T(8,128)(2,1)S(1)}, bf16[128,32]{0,1:T(8,128)(2,1)}, u32[]{:S(2)}) copy-start(bf16[128,32]{0,1:T(8,128)(2,1)} %param.15) | copy-start | bytes 24580
  809.1 14.4 copy-start.2
  823.5 37.7 %copy-start.7 = (bf16[128,32]{0,1:T(8,128)(2,1)S(1)}, bf16[128,32]{0,1:T(8,128)(2,1)}, u32[]{:S(2)}) copy-start(bf16[128,32]{0,1:T(8,128)(2,1)} %param.13) | copy-start | bytes 24580
  823.5 494.7 %all-reduce.3.cloned.1.call-start = ((), (), s32[]{:S(2)}) async-start(), calls=%async_computation.5 | async-start | bytes 1048576 | tf_op jit(solution)/shard_map/psum | solution.py:52
  1272.5 98.7 %copy-start.5 = (f32[32]{0:T(128)S(1)}, f32[32]{0:T(128)}, u32[]{:S(2)}) copy-start(f32[32]{0:T(128)} %param.18) | copy-start | bytes 388
  1282.0 88.1 %all-reduce.5.cloned.1.call-start = ((), (), s32[]{:S(2)}) async-start(), calls=%async_computation.6 | async-start | bytes 1048576 | tf_op jit(solution)/shard_map/psum | solution.py:55
  1331.5 612.2 %all-gather.8.cloned.1.call-start = ((), (), s32[]{:S(2)}) async-start(), calls=%async_computation.7 | async-start | bytes 41943040 | tf_op jit(solution)/shard_map/all_gather | solution.py:59
  1371.3 11.1 copy-start.3
  1382.4 561.3 %copy-start.8 = (bf16[128,32]{0,1:T(8,128)(2,1)S(1)}, bf16[128,32]{0,1:T(8,128)(2,1)}, u32[]{:S(2)}) copy-start(bf16[128,32]{0,1:T(8,128)(2,1)} %param.19) | copy-start | bytes 24580
  1943.7 33.4 %copy-start.1 = (bf16[128,32]{0,1:T(8,128)(2,1)S(1)}, bf16[128,32]{0,1:T(8,128)(2,1)}, u32[]{:S(2)}) copy-start(bf16[128,32]{0,1:T(8,128)(2,1)} %param.16) | copy-start | bytes 24580
Sparse Core Ops, SparseCore 0:
  8.9 564.0 all-gather.3
  823.6 26.7 all-gather.5
  1282.1 36.0 all-reduce.2
  1331.6 38.4 all-reduce.4
  1382.5 561.1 all-gather.7
where the time goes:
time: 1990 us; the launch traced here: 1980 us
  waiting for transfers between devices  1170 us (59%)
  blocking collectives  383 us (19%)
  matrix products  224 us (11%)
  local copies, waits for them, and re-layouts  115 us (6%)
  other arithmetic  82.3 us (4%)
    all_gather x1, waiting for transfers between devices, local(): lax.all_gather(pair, 'gz', axis=0, tiled=True).astype(jnp.float32)  565 us
    all_gather x1, waiting for transfers between devices, local(): normed_mix = lax.all_gather(local_mix, 'gz', axis=0, tiled=True)  526 us
    all_to_all x1, blocking collectives, local(): lax.all_to_all(full_product, 'gx', split_axis=2, concat_axis=0, tiled=True)  191 us
    dot_general x4, matrix products, project(): jnp.einsum('cik,ch->hik', normed, weight, preferred_element_type=jnp.floa...  150 us
    all_to_all x1, blocking collectives, local(): lax.all_to_all(right_rows, 'gx', split_axis=0, concat_axis=2, tiled=True)  97.4 us
    all_to_all x1, blocking collectives, local(): lax.all_to_all(left_rows, 'gx', split_axis=0, concat_axis=2, tiled=True)  94.8 us
  transfers between devices with their start and end apart: 5, of which 4 were waited for; matrix products, arithmetic and copies ran while one was open for 7% of the time, Pallas kernels for 0%

commit v1 on v0

--- a/solution.py
+++ b/solution.py
@@ -18,6 +18,15 @@
     out_gain,
     w_out,
 ):
+
+    def wait_the_space(packet):
+        d_next = lax.axis_size("gx")
+        carry_out = jnp.split(packet, d_next, axis=2)
+        even = jnp.stack(carry_out)
+        t_next = lax.all_to_all(even, "gx", 0, 0)
+        left_arr = jnp.concatenate(t_next, axis=0)
+        return left_arr
+
     gathered = lax.all_gather(pair, "gz", axis=0, tiled=True).astype(jnp.float32)
     average = jnp.mean(gathered, axis=0)
     centered = gathered - average
@@ -47,7 +56,7 @@
         (((2,), (2,)), ((0,), (0,))),
         preferred_element_type=jnp.float32,
     )
-    mixed_sum = lax.all_to_all(full_product, "gx", split_axis=2, concat_axis=0, tiled=True)
+    mixed_sum = wait_the_space(full_product)
     channel_count = lax.axis_size("gz") * mixed_sum.shape[0]
     sum_terms = lax.psum(jnp.sum(mixed_sum, axis=0), "gz")
     mix_average = sum_terms / channel_count

time: 1990 us -> 1960 us (0.985)
  local copies, waits for them, and re-layouts: 115 us -> 84.3 us
    all_to_all x1 -> x0, local copies, waits for them, and re-layouts: 20.2 us -> none  [local(): lax.all_to_all(full_product, 'gx', split_axis=2, concat_axis=0, tiled=True)]
where the time goes in v1:
time: 1960 us; the launch traced here: 1950 us
  waiting for transfers between devices  1170 us (60%)
  blocking collectives  376 us (19%)
  matrix products  224 us (11%)
  local copies, waits for them, and re-layouts  84.3 us (4%)
  other arithmetic  84 us (4%)
    all_gather x1, waiting for transfers between devices, local(): lax.all_gather(pair, 'gz', axis=0, tiled=True).astype(jnp.float32)  565 us
    all_gather x1, waiting for transfers between devices, local(): normed_mix = lax.all_gather(local_mix, 'gz', axis=0, tiled=True)  525 us
    all_to_all x1, blocking collectives, wait_the_space(): t_next = lax.all_to_all(even, 'gx', 0, 0)  184 us
    dot_general x4, matrix products, project(): jnp.einsum('cik,ch->hik', normed, weight, preferred_element_type=jnp.floa...  149 us
    all_to_all x1, blocking collectives, local(): lax.all_to_all(right_rows, 'gx', split_axis=0, concat_axis=2, tiled=True)  97.4 us
    all_to_all x1, blocking collectives, local(): lax.all_to_all(left_rows, 'gx', split_axis=0, concat_axis=2, tiled=True)  94.8 us
  transfers between devices with their start and end apart: 5, of which 4 were waited for; matrix products, arithmetic and copies ran while one was open for 7% of the time, Pallas kernels for 0%

profile of v1, /device:TPU:0, one launch (start us, length us, event | category | flops | bytes accessed | tf_op | source)
XLA Modules:
  0.0 1947.9 jit_solution(2516835165825366884)
XLA Ops:
  8.4 564.6 %all-gather.4.cloned.1.call-done = bf16[128,512,256]{2,1,0:T(8,128)(2,1)} async-done(((bf16[32,512,256]{2,1,0:T(8,128)(2,1)}), bf16[128,512,256]{2,1,0:T(8,128)(2,1)}) %all-gather.4.cloned.1.call-update) | async-done | bytes 33554448 | tf_op jit(solution)/shard_map/all_gather | solution.py:30
  573.0 11.4 convert_reduce_fusion
  584.5 11.7 fusion.2
  596.2 23.0 %fusion.4 = bf16[128,512,256]{2,1,0:T(8,128)(2,1)} fusion(bf16[128,512,256]{2,1,0:T(8,128)(2,1)} %all-gather.4.cloned.1.call-done, f32[128]{0:T(128)S(1)} %copy-done.4, f32[512,256]{1,0:T(8,128)S(1)} %add_rsqrt_fusion.1, f32[512,256]{1,0:T(8,128)S(1)} %broadcast_multiply_fusion.1), kind=kLoop, calls=%fused_computation.6 | loop fusion | flops 83886080 | bytes 68157952 | tf_op jit(solution)/shard_map/convert_element_type | solution.py:34
  619.2 35.7 %fusion.11 = f32[512,256,32]{1,2,0:T(8,128)} fusion(bf16[128,512,256]{2,1,0:T(8,128)(2,1)} %fusion.4, bf16[128,32]{0,1:T(8,128)(2,1)S(1)} %copy-done), kind=kOutput, calls=%fused_computation.13 | convolution fusion | flops 1073741824 | bytes 50339840 | tf_op jit(solution)/shard_map/cik,ch->hik/dot_general | solution.py:38
  654.9 38.1 %fusion.26 = bf16[32,512,256]{2,0,1:T(8,128)(2,1)} fusion(bf16[128,512,256]{2,1,0:T(8,128)(2,1)} %fusion.4, f32[512,256,32]{1,2,0:T(8,128)} %fusion.11, f32[512,256]{1,0:T(8,128)S(1)} %convert_element_type.23, bf16[128,32]{0,1:T(8,128)(2,1)S(1)} %copy-done.6), kind=kOutput, calls=%fused_computation.30 | convolution fusion | flops 1098907648 | bytes 59252736 | tf_op jit(solution)/shard_map/cik,ch->hik/dot_general | solution.py:38
  693.0 11.4 copy.27
  704.4 97.4 %all_to_all.41 = bf16[32,512,256]{2,1,0:T(8,128)(2,1)S(1)} all-to-all(bf16[32,512,256]{2,1,0:T(8,128)(2,1)} %copy.27), channel_id=1, replica_groups=mesh['gx'=4,'gy'=2,'gz'=4] {'gx'}, dimensions={0} | all-to-all | bytes 16777216 | tf_op jit(solution)/shard_map/all_to_all | solution.py:51
  809.0 14.3 all_to_all.36
  823.4 37.6 %fusion.7 = f32[512,256,32]{1,2,0:T(8,128)} fusion(bf16[128,512,256]{2,1,0:T(8,128)(2,1)} %fusion.4, bf16[128,32]{0,1:T(8,128)(2,1)S(1)} %copy-done.2), kind=kOutput, calls=%fused_computation.9 | convolution fusion | flops 1073741824 | bytes 50339840 | tf_op jit(solution)/shard_map/cik,ch->hik/dot_general | solution.py:38
  861.0 38.1 %fusion.23 = bf16[32,512,256]{2,0,1:T(8,128)(2,1)} fusion(bf16[128,512,256]{2,1,0:T(8,128)(2,1)} %fusion.4, f32[512,256,32]{1,2,0:T(8,128)} %fusion.7, f32[512,256]{1,0:T(8,128)S(1)} %convert_element_type.23, bf16[128,32]{0,1:T(8,128)(2,1)S(1)} %copy-done.7), kind=kOutput, calls=%fused_computation.29 | convolution fusion | flops 1098907648 | bytes 59252736 | tf_op jit(solution)/shard_map/cik,ch->hik/dot_general | solution.py:38
  899.2 11.4 copy.23
  910.5 94.8 %all_to_all.42 = bf16[32,512,256]{2,1,0:T(8,128)(2,1)S(1)} all-to-all(bf16[32,512,256]{2,1,0:T(8,128)(2,1)} %copy.23), channel_id=1, replica_groups=mesh['gx'=4,'gy'=2,'gz'=4] {'gx'}, dimensions={0} | all-to-all | bytes 16777216 | tf_op jit(solution)/shard_map/all_to_all | solution.py:50
  1012.6 14.3 all_to_all.32
  1027.0 17.0 fusion.35
  1051.9 184.0 %all_to_all.43 = f32[4,8,512,256]{3,2,1,0:T(8,128)} all-to-all(f32[4,8,512,256]{3,2,1,0:T(8,128)S(1)} %pad_maximum_fusion), channel_id=1, replica_groups=mesh['gx'=4,'gy'=2,'gz'=4] {'gx'}, dimensions={0} | all-to-all | bytes 33554432 | tf_op jit(solution)/shard_map/all_to_all | solution.py:26
  1243.7 36.0 %all-reduce.3.cloned.1.call-done = f32[512,256]{1,0:T(8,128)} async-done(((f32[512,256]{1,0:T(8,128)}), f32[512,256]{1,0:T(8,128)}) %all-reduce.3.cloned.1.call-update) | async-done | bytes 524304 | tf_op jit(solution)/shard_map/psum | solution.py:61
  1280.8 8.5 multiply_reduce_fusion
  1289.4 38.6 %all-reduce.5.cloned.1.call-done = f32[512,256]{1,0:T(8,128)} async-done(((f32[512,256]{1,0:T(8,128)}), f32[512,256]{1,0:T(8,128)}) %all-reduce.5.cloned.1.call-update) | async-done | bytes 524304 | tf_op jit(solution)/shard_map/psum | solution.py:64
  1329.1 17.1 fusion.17
  1346.2 36.0 %fusion.5 = f32[512,256,32]{1,2,0:T(8,128)} fusion(bf16[128,512,256]{2,1,0:T(8,128)(2,1)} %fusion.4, bf16[128,32]{0,1:T(8,128)(2,1)S(1)} %copy-done.3), kind=kOutput, calls=%fused_computation.7 | convolution fusion | flops 1073741824 | bytes 50339840 | tf_op jit(solution)/shard_map/cij,cd->dij/dot_general | solution.py:47
  1382.2 525.3 %all-gather.8.cloned.1.call-done = bf16[128,512,256]{2,0,1:T(8,128)(2,1)} async-done(((bf16[32,512,256]{2,0,1:T(8,128)(2,1)}), bf16[128,512,256]{2,0,1:T(8,128)(2,1)}) %all-gather.8.cloned.1.call-update) | async-done | bytes 33554448 | tf_op jit(solution)/shard_map/all_gather | solution.py:68
  1907.6 21.8 %fusion.22 = bf16[32,512,256]{2,0,1:T(8,128)(2,1)} fusion(bf16[128,512,256]{2,0,1:T(8,128)(2,1)} %all-gather.8.cloned.1.call-done, f32[512,256,32]{1,2,0:T(8,128)} %fusion.5, bf16[128,32]{0,1:T(8,128)(2,1)S(1)} %copy-done.8), kind=kOutput, calls=%fused_computation.28 | convolution fusion | flops 1094713344 | bytes 58728448 | tf_op jit(solution)/shard_map/hij,hd->dij/dot_general | solution.py:69
  1929.4 11.5 copy.30
  (39 shorter events, 34.6 us)
Async XLA Ops:
  6.5 612.7 %copy-start = (bf16[128,32]{0,1:T(8,128)(2,1)S(1)}, bf16[128,32]{0,1:T(8,128)(2,1)}, u32[]{:S(2)}) copy-start(bf16[128,32]{0,1:T(8,128)(2,1)} %param.16) | copy-start | bytes 24580
  6.5 566.5 %all-gather.4.cloned.1.call-start = ((), (), s32[]{:S(2)}) async-start(), calls=%async_computation.3 | async-start | bytes 41943040 | tf_op jit(solution)/shard_map/all_gather | solution.py:30
  7.3 1019.7 %all-gather.6.cloned.1.call-start = ((), (), s32[]{:S(2)}) async-start(), calls=%async_computation.4 | async-start | bytes 25165824 | tf_op jit(solution)/shard_map/all_gather | solution.py:55
  584.5 11.8 copy-start.4
  619.2 35.7 %copy-start.6 = (bf16[128,32]{0,1:T(8,128)(2,1)S(1)}, bf16[128,32]{0,1:T(8,128)(2,1)}, u32[]{:S(2)}) copy-start(bf16[128,32]{0,1:T(8,128)(2,1)} %param.15) | copy-start | bytes 24580
  809.0 14.4 copy-start.2
  823.4 37.7 %copy-start.7 = (bf16[128,32]{0,1:T(8,128)(2,1)S(1)}, bf16[128,32]{0,1:T(8,128)(2,1)}, u32[]{:S(2)}) copy-start(bf16[128,32]{0,1:T(8,128)(2,1)} %param.13) | copy-start | bytes 24580
  823.4 456.3 %all-reduce.3.cloned.1.call-start = ((), (), s32[]{:S(2)}) async-start(), calls=%async_computation.5 | async-start | bytes 1048576 | tf_op jit(solution)/shard_map/psum | solution.py:61
  1236.0 93.1 %copy-start.5 = (f32[32]{0:T(128)S(1)}, f32[32]{0:T(128)}, u32[]{:S(2)}) copy-start(f32[32]{0:T(128)} %param.18) | copy-start | bytes 388
  1243.7 84.3 %all-reduce.5.cloned.1.call-start = ((), (), s32[]{:S(2)}) async-start(), calls=%async_computation.6 | async-start | bytes 1048576 | tf_op jit(solution)/shard_map/psum | solution.py:64
  1289.3 618.2 %all-gather.8.cloned.1.call-start = ((), (), s32[]{:S(2)}) async-start(), calls=%async_computation.7 | async-start | bytes 41943040 | tf_op jit(solution)/shard_map/all_gather | solution.py:68
  1329.1 17.1 copy-start.3
  1346.2 561.3 %copy-start.8 = (bf16[128,32]{0,1:T(8,128)(2,1)S(1)}, bf16[128,32]{0,1:T(8,128)(2,1)}, u32[]{:S(2)}) copy-start(bf16[128,32]{0,1:T(8,128)(2,1)} %param.19) | copy-start | bytes 24580
  1907.6 33.4 %copy-start.1 = (bf16[128,32]{0,1:T(8,128)(2,1)S(1)}, bf16[128,32]{0,1:T(8,128)(2,1)}, u32[]{:S(2)}) copy-start(bf16[128,32]{0,1:T(8,128)(2,1)} %param.16) | copy-start | bytes 24580
Sparse Core Ops, SparseCore 0:
  8.9 564.0 all-gather.3
  823.5 26.7 all-gather.5
  1243.8 35.8 all-reduce.2
  1289.4 38.4 all-reduce.4
  1346.3 561.1 all-gather.7
